TPU v7x, 32 devices: a whole 2x2x4 slice. The times are simulated.
32 devices in a mesh: row: 16 (over z, x, core), col: 2 (over y).
Axes of the slice: x: 2, y: 2, z: 4, core: 2. Of those that a mesh axis runs over, the one named last changes fastest.
Arguments:
- features: bfloat16 [4096, 440], P(('row', 'col')), may hold values from -1 to 1
- coeffs: bfloat16 [4096, 144], P(('row', 'col')), may hold values from -0.375 to 0.375
- targets: float32 [4096, 144], P(('row', 'col')), may hold values from -6 to 6
Outputs:
- residual: float32 [4096, 144], P(('row', 'col'))
All inputs are finite; a program needn't handle non-finite values.
Results may differ from a plain program's by a relative error of at most 0.0012.
Values may be sent and summed in bfloat16 or wider, within the bound.
No kernel may reach another device: no remote copies, remote signals or barrier semaphores. Data moves between devices by JAX's collectives and lax.ppermute only.
A program may use at most 64 MiB of HBM per device.

v0:
```python
import jax
import jax.numpy as jnp
from jax import lax
from jax.sharding import PartitionSpec as P


def frame_squares(block):
    return jnp.sum(jnp.square(block.astype(jnp.float32)), axis=1)


def sweep(queries, keys, col_weights):
    rows = queries.shape[0]
    count = keys.shape[0]
    target = max(8, (1 << 20) // count)
    piece = rows
    while piece > target and piece % 2 == 0:
        piece = piece // 2
    steps = rows // piece
    key_squares = frame_squares(keys)
    query_squares = frame_squares(queries)
    query_blocks = queries.reshape(steps, piece, queries.shape[1])
    square_blocks = query_squares.reshape(steps, piece)

    def kernel_rows(query_part, square_part):
        inner = lax.dot_general(
            query_part, keys, (((1,), (1,)), ((), ())), preferred_element_type=jnp.float32
        )
        distance = jnp.sqrt(
            jnp.maximum(square_part[:, None] + key_squares[None, :] - 2.0 * inner, 0.0)
        )
        return jnp.exp(-distance).astype(jnp.bfloat16)

    def advance(carry, items):
        kernel = kernel_rows(items[0], items[1])
        return (carry, jnp.dot(kernel, col_weights, preferred_element_type=jnp.float32))

    unused, direct = lax.scan(advance, jnp.zeros((), jnp.float32), (query_blocks, square_blocks))
    return (direct.reshape(rows, col_weights.shape[1]), None)


def column_frames(features, coeffs):
    keys, weights = (
        lax.all_gather(features, "row", axis=0, tiled=True),
        lax.all_gather(coeffs, "row", axis=0, tiled=True),
    )
    return (keys, weights)


def per_device(features, coeffs, targets):
    queries = lax.all_gather(features, "col", axis=0, tiled=True)
    keys, weights = column_frames(features, coeffs)
    direct, unused = sweep(queries, keys, weights)
    summed = lax.psum_scatter(direct, "col", scatter_dimension=0, tiled=True)
    return summed - targets


def solution(mesh):
    in_specs = (P(("row", "col"), None), P(("row", "col"), None), P(("row", "col"), None))
    out_specs = P(("row", "col"), None)
    return jax.shard_map(
        per_device, mesh=mesh, in_specs=in_specs, out_specs=out_specs, check_vma=False
    )
```

profile of v0, /device:TPU:0, one launch (start us, length us, event | category | flops | bytes accessed | tf_op | source)
XLA Modules:
  0.0 76.4 jit_solution(7553263874283629161)
XLA Ops:
  6.5 0.0 all-gather.2.cloned.1.call-start
  6.5 0.7 all-gather.2.cloned.1.call-update
  7.3 0.0 reduce-scatter.2.cloned.1.call-start
  7.3 7.1 %all_gather.9 = bf16[256,440]{0,1:T(8,128)(2,1)S(1)} all-gather(bf16[128,440]{0,1:T(8,128)(2,1)} %param.3), channel_id=1, replica_groups=mesh['row'=16,'col'=2] {'col'}, dimensions={0}, use_global_device_ids=true | all-gather | bytes 337920 | tf_op jit(solution)/shard_map/all_gather | solution.py:50
  14.4 0.1 multiply_reduce_fusion.1
  14.5 24.4 %all_gather.11 = bf16[2048,144]{0,1:T(8,128)(2,1)S(1)} all-gather(bf16[128,144]{0,1:T(8,128)(2,1)} %param.4), channel_id=1, replica_groups=mesh['row'=16,'col'=2] {'row'}, dimensions={0}, use_global_device_ids=true | all-gather | bytes 626688 | tf_op jit(solution)/shard_map/all_gather | solution.py:44
  38.9 14.8 %all-gather.2.cloned.1.call-done = bf16[2048,440]{0,1:T(8,128)(2,1)} async-done(((bf16[128,440]{0,1:T(8,128)(2,1)}), bf16[2048,440]{0,1:T(8,128)(2,1)}) %all-gather.2.cloned.1.call-update) | async-done | bytes 1802256 | tf_op jit(solution)/shard_map/all_gather | solution.py:43
  53.6 0.0 copy-start
  53.6 2.0 %multiply_reduce_fusion = f32[2048]{0:T(1024)S(1)} fusion(bf16[2048,440]{0,1:T(8,128)(2,1)} %all-gather.2.cloned.1.call-done), kind=kLoop, calls=%fused_computation | loop fusion | flops 2701312 | bytes 1810432 | tf_op jit(solution)/shard_map/reduce_sum | solution.py:8
  55.6 0.0 copy-done
  55.7 0.0 copy-start.1
  55.7 2.3 %fusion.6 = f32[256,144]{0,1:T(8,128)} fusion(bf16[2048,144]{0,1:T(8,128)(2,1)S(1)} %all_gather.11, bf16[256,440]{0,1:T(8,128)(2,1)S(1)} %all_gather.9, bf16[2048,440]{0,1:T(8,128)(2,1)S(1)} %copy-done, f32[2048]{0:T(1024)S(1)} %multiply_reduce_fusion, f32[256]{0:T(256)S(1)} %multiply_reduce_fusion.1), kind=kOutput, calls=%fused_computation.8 | convolution fusion | flops 615514112 | bytes 2774016 | tf_op jit(solution)/shard_map/while/body/eval_jaxpr/dot_general | solution.py:35
  58.0 0.0 reduce-scatter.2.cloned.1.call-update
  58.0 10.0 %reduce-scatter.2.cloned.1.call-done = f32[128,144]{0,1:T(8,128)} async-done(((f32[256,144]{0,1:T(8,128)}), f32[128,144]{0,1:T(8,128)}) %reduce-scatter.2.cloned.1.call-update) | async-done | bytes 73744 | tf_op jit(solution)/shard_map/reduce_scatter | solution.py:53
  68.0 0.0 copy-done.1
  68.0 1.5 %sub.8 = f32[128,144]{0,1:T(8,128)} subtract(f32[128,144]{0,1:T(8,128)} %reduce-scatter.2.cloned.1.call-done, f32[128,144]{0,1:T(8,128)S(1)} %copy-done.1) | non-fusion elementwise | flops 18432 | bytes 221184 | tf_op jit(solution)/shard_map/sub | solution.py:54
Async XLA Ops:
  6.5 47.1 %all-gather.2.cloned.1.call-start = ((), (), s32[]{:S(2)}) async-start(), calls=%async_computation.1 | async-start | bytes 1914880 | tf_op jit(solution)/shard_map/all_gather | solution.py:43
  7.3 60.7 %reduce-scatter.2.cloned.1.call-start = ((), (), s32[]{:S(2)}) async-start(), calls=%async_computation.2 | async-start | bytes 221184 | tf_op jit(solution)/shard_map/reduce_scatter | solution.py:53
  53.6 2.0 %copy-start = (bf16[2048,440]{0,1:T(8,128)(2,1)S(1)}, bf16[2048,440]{0,1:T(8,128)(2,1)}, u32[]{:S(2)}) copy-start(bf16[2048,440]{0,1:T(8,128)(2,1)} %all-gather.2.cloned.1.call-done) | copy-start | bytes 5406724
  55.7 12.3 %copy-start.1 = (f32[128,144]{0,1:T(8,128)S(1)}, f32[128,144]{0,1:T(8,128)}, u32[]{:S(2)}) copy-start(f32[128,144]{0,1:T(8,128)} %param.5) | copy-start | bytes 221188
Sparse Core Ops, SparseCore 0:
  9.5 44.1 all-gather.1
  58.1 9.8 reduce-scatter.1
where the time goes:
time: 76.5 us; the launch traced here: 76.4 us
  blocking collectives  31.5 us (41%)
  waiting for transfers between devices  25.5 us (33%)
  between operations  13.4 us (18%)
  other arithmetic  3.61 us (5%)
  matrix products  2.33 us (3%)
    all_gather x1, blocking collectives, column_frames(): lax.all_gather(coeffs, 'row', axis=0, tiled=True)  24.4 us
    all_gather x1, waiting for transfers between devices, column_frames(): lax.all_gather(features, 'row', axis=0, tiled=True)  14.8 us
    reduce_scatter x1, waiting for transfers between devices, per_device(): summed = lax.psum_scatter(direct, 'col', scatter_dimension=0, tiled=True)  9.97 us
    all_gather x1, blocking collectives, per_device(): queries = lax.all_gather(features, 'col', axis=0, tiled=True)  7.07 us
    dot_general x1, matrix products, advance(): jnp.dot(kernel, col_weights, preferred_element_type=jnp.float32)  2.33 us
    reduce_sum x2, other arithmetic, frame_squares(): return jnp.sum(jnp.square(block.astype(jnp.float32)), axis=1)  2.09 us
  transfers between devices with their start and end apart: 2, of which 2 were waited for; matrix products, arithmetic and copies ran while one was open for 0% of the time, Pallas kernels for 0%

commit v1 on v0

v1 whole, which is shorter than its diff:
```python
import functools
import math

import jax
import jax.numpy as jnp
from jax import lax
from jax.experimental import pallas as pl
from jax.experimental.pallas import tpu as pltpu
from jax.sharding import PartitionSpec as P

AXES = ("row", "col")
NEAR_BYTES = 2 << 20
LOG2E = math.log2(math.e)


def kernel_products(queries, keys, weights):
    nq, nk = len(queries), len(keys)
    outs = weights[0].shape[0]
    step = 2 if nk % 2 == 0 else 1

    def body(*refs):
        q_refs, k_refs, w_refs = refs[:nq], refs[nq:nq + nk], refs[nq + nk:nq + 2 * nk]
        out_refs = refs[nq + 2 * nk:]
        lhs, lhs_sq = [], []
        for q_ref in q_refs:
            q = q_ref[...].T
            q32 = q.astype(jnp.float32)
            lhs.append((q32 * -2.0).astype(jnp.bfloat16))
            lhs_sq.append(jnp.sum(q32 * q32, axis=1, keepdims=True))
        acc = [None] * nq
        for k in range(0, nk, step):
            rhs = jnp.concatenate([k_refs[k + s][...] for s in range(step)], axis=1)
            w = jnp.concatenate([w_refs[k + s][...] for s in range(step)], axis=1)
            rhs32 = rhs.astype(jnp.float32)
            rhs_sq = jnp.sum(rhs32 * rhs32, axis=0, keepdims=True)
            for i in range(nq):
                inner = jnp.dot(lhs[i], rhs, preferred_element_type=jnp.float32)
                d2 = jnp.maximum((inner + rhs_sq) + lhs_sq[i], 1e-30)
                kern = jnp.exp2((d2 * -LOG2E) * lax.rsqrt(d2)).astype(jnp.bfloat16)
                part = lax.dot_general(
                    w, kern, (((1,), (1,)), ((), ())), preferred_element_type=jnp.float32
                )
                acc[i] = part if acc[i] is None else acc[i] + part
        for i in range(nq):
            out_refs[i][...] = acc[i].astype(out_refs[i].dtype)

    held = [*queries, *keys, *weights]
    shapes = [
        ((outs, q.shape[1]), jnp.float32 if i == 0 else jnp.bfloat16)
        for i, q in enumerate(queries)
    ]
    vmem = pl.BlockSpec(memory_space=pltpu.VMEM)
    if sum(a.size * a.dtype.itemsize for a in held) <= NEAR_BYTES:
        held = [pltpu.with_memory_space_constraint(a, pltpu.VMEM) for a in held]
        shapes = [pltpu.VMEM(*s) for s in shapes]
    else:
        shapes = [jax.ShapeDtypeStruct(*s) for s in shapes]
    return pl.pallas_call(
        body,
        out_shape=shapes,
        in_specs=[vmem] * (nq + 2 * nk),
        out_specs=[vmem] * nq,
        name="products",
    )(*held)


def per_device(rows, cols, features, coeffs, targets):
    total = rows * cols
    core, xbit, z = cols, 2 * cols, 4 * cols

    def swap(value, bits):
        return lax.ppermute(value, AXES, [(i, i ^ bits) for i in range(total)])

    mine = features.T
    coef = coeffs.T
    queries = [mine]
    order = [0]
    bit = rows // 8
    while bit >= 1:
        queries = queries + [swap(q, bit * z) for q in queries]
        order = order + [o ^ (bit * z) for o in order]
        bit = bit // 2
    keys, weights = [mine], [coef]
    for plane in range(1, 2 * cols):
        bits = (plane // cols) * xbit + plane % cols
        keys.append(swap(mine, bits))
        weights.append(swap(coef, bits))
    keys = keys + [swap(k, core) for k in keys]
    weights = weights + [swap(w, core) for w in weights]

    parts = kernel_products(queries, keys, weights)
    total_part = parts[0] - targets.T
    for bits, part in list(zip(order, parts))[1:]:
        total_part = total_part + swap(part, bits).astype(jnp.float32)
    return total_part.T


def solution(mesh):
    body = functools.partial(per_device, mesh.shape["row"], mesh.shape["col"])
    spec = P(AXES, None)
    return jax.shard_map(
        body, mesh=mesh, in_specs=(spec, spec, spec), out_specs=spec, check_vma=False
    )
```

time: 76.5 us -> 39.2 us (0.51)
  blocking collectives: 31.5 us -> 0 us
  starting transfers between devices: 0.04 us -> 18.3 us
  between operations: 13.4 us -> 0.04 us
  waiting for transfers between devices: 25.5 us -> 16.7 us
  other arithmetic: 3.61 us -> 0.66 us
  matrix products: 2.33 us -> 0 us
  Pallas kernels: 0 us -> 1.67 us
  local copies, waits for them, and re-layouts: 0.03 us -> 1.67 us
    all_gather x2 -> x0, blocking collectives: 31.5 us -> none  [the longest x1 24.4 us: column_frames(): lax.all_gather(coeffs, 'row', axis=0, tiled=True)]
    ppermute x0 -> x20, starting transfers between devices: none -> 18.3 us  [swap(): return lax.ppermute(value, AXES, [(i, i ^ bits) for i in range(total)])]
    ppermute x0 -> x20, waiting for transfers between devices: none -> 16.7 us  [swap(): return lax.ppermute(value, AXES, [(i, i ^ bits) for i in range(total)])]
    all_gather x1 -> x0, waiting for transfers between devices: 14.8 us -> none  [column_frames(): lax.all_gather(features, 'row', axis=0, tiled=True)]
    reduce_scatter x1 -> x0, waiting for transfers between devices: 9.97 us -> none  [per_device(): summed = lax.psum_scatter(direct, 'col', scatter_dimension=0, tiled=True)]
    dot_general x1 -> x0, matrix products: 2.33 us -> none  [advance(): jnp.dot(kernel, col_weights, preferred_element_type=jnp.float32)]
    reduce_sum x2 -> x0, other arithmetic: 2.09 us -> none  [frame_squares(): return jnp.sum(jnp.square(block.astype(jnp.float32)), axis=1)]
    pallas_call x0 -> x1, Pallas kernels: none -> 1.67 us  [kernel_products(): pl.pallas_call(body, out_shape=shapes, in_specs=[vmem] * (nq + 2 * nk), o...]
  transfers between devices with their start and end apart: 2 -> 20, of which waited for: 2 -> 9; matrix products, arithmetic and copies ran while one was open for 0% -> 0% of each run, Pallas kernels for 0% -> 0%
where the time goes in v1:
time: 39.2 us; the launch traced here: 39 us
  starting transfers between devices  18.3 us (47%)
  waiting for transfers between devices  16.7 us (43%)
  local copies, waits for them, and re-layouts  1.67 us (4%)
  Pallas kernels  1.67 us (4%)
  other arithmetic  0.66 us (2%)
    ppermute x20, starting transfers between devices, swap(): return lax.ppermute(value, AXES, [(i, i ^ bits) for i in range(total)])  18.3 us
    ppermute x20, waiting for transfers between devices, swap(): return lax.ppermute(value, AXES, [(i, i ^ bits) for i in range(total)])  16.7 us
    pallas_call x1, Pallas kernels, kernel_products(): pl.pallas_call(body, out_shape=shapes, in_specs=[vmem] * (nq + 2 * nk), o...  1.67 us
    unnamed x6, local copies, waits for them, and re-layouts  1.67 us
  transfers between devices with their start and end apart: 20, of which 9 were waited for; matrix products, arithmetic and copies ran while one was open for 0% of the time, Pallas kernels for 0%

profile of v1, /device:TPU:0, one launch (start us, length us, event | category | flops | bytes accessed | tf_op | source)
XLA Modules:
  0.0 39.0 jit_solution(10817901002170279097)
XLA Ops:
  0.0 3.9 %collective-permute-start.12 = (bf16[144,128]{1,0:T(8,128)(2,1)}, bf16[144,128]{1,0:T(8,128)(2,1)S(1)}, u32[]{:S(2)}, u32[]{:S(2)}) collective-permute-start(bf16[144,128]{1,0:T(8,128)(2,1)} %bitcast.22), channel_id=1, source_target_pairs={{0,5},{1,4},{2,7},{3,6},{4,1},{5,0},{6,3},{7,2},{8,13},{9,12},{10,... | collective-permute-start | bytes 110600 | tf_op jit(solution)/shard_map/ppermute | solution.py:72
  3.9 0.5 %collective-permute-start.11 = (bf16[144,128]{1,0:T(8,128)(2,1)}, bf16[144,128]{1,0:T(8,128)(2,1)S(1)}, u32[]{:S(2)}, u32[]{:S(2)}) collective-permute-start(bf16[144,128]{1,0:T(8,128)(2,1)} %bitcast.23), channel_id=1, source_target_pairs={{0,4},{1,5},{2,6},{3,7},{4,0},{5,1},{6,2},{7,3},{8,12},{9,13},{10,... | collective-permute-start | bytes 110600 | tf_op jit(solution)/shard_map/ppermute | solution.py:72
  4.5 0.0 collective-permute-start.10
  4.5 0.0 collective-permute-start.13
  4.5 1.6 %collective-permute-done.12.refs_15_ = bf16[144,128]{1,0:T(8,128)(2,1)S(1)} collective-permute-done((bf16[144,128]{1,0:T(8,128)(2,1)}, bf16[144,128]{1,0:T(8,128)(2,1)S(1)}, u32[]{:S(2)}, u32[]{:S(2)}) %collective-permute-start.12) | collective-permute-done | bytes 36896 | tf_op jit(solution)/shard_map/ppermute | solution.py:72
  6.1 0.0 collective-permute-start.16
  6.1 2.0 %collective-permute-done.11.refs_14_ = bf16[144,128]{1,0:T(8,128)(2,1)S(1)} collective-permute-done((bf16[144,128]{1,0:T(8,128)(2,1)}, bf16[144,128]{1,0:T(8,128)(2,1)S(1)}, u32[]{:S(2)}, u32[]{:S(2)}) %collective-permute-start.11) | collective-permute-done | bytes 36896 | tf_op jit(solution)/shard_map/ppermute | solution.py:72
  8.1 0.0 collective-permute-start.15
  8.1 0.5 %collective-permute-done.10.refs_13_ = bf16[144,128]{1,0:T(8,128)(2,1)S(1)} collective-permute-done((bf16[144,128]{1,0:T(8,128)(2,1)}, bf16[144,128]{1,0:T(8,128)(2,1)S(1)}, u32[]{:S(2)}, u32[]{:S(2)}) %collective-permute-start.10) | collective-permute-done | bytes 36896 | tf_op jit(solution)/shard_map/ppermute | solution.py:72
  8.6 0.0 collective-permute-start.14
  8.6 0.5 %collective-permute-start.6 = (bf16[440,128]{1,0:T(8,128)(2,1)}, bf16[440,128]{1,0:T(8,128)(2,1)S(1)}, u32[]{:S(2)}, u32[]{:S(2)}) collective-permute-start(bf16[440,128]{1,0:T(8,128)(2,1)} %bitcast.14), channel_id=1, source_target_pairs={{0,2},{1,3},{2,0},{3,1},{4,6},{5,7},{6,4},{7,5},{8,10},{9,11},{10,... | collective-permute-start | bytes 337928 | tf_op jit(solution)/shard_map/ppermute | solution.py:72
  9.1 0.0 collective-permute-done.13.refs_16_
  9.1 1.4 %collective-permute-start.5 = (bf16[440,128]{1,0:T(8,128)(2,1)}, bf16[440,128]{1,0:T(8,128)(2,1)S(1)}, u32[]{:S(2)}, u32[]{:S(2)}) collective-permute-start(bf16[440,128]{1,0:T(8,128)(2,1)} %bitcast.15), channel_id=1, source_target_pairs={{0,5},{1,4},{2,7},{3,6},{4,1},{5,0},{6,3},{7,2},{8,13},{9,12},{10,... | collective-permute-start | bytes 337928 | tf_op jit(solution)/shard_map/ppermute | solution.py:72
  10.6 0.0 collective-permute-done.16.refs_19_
  10.6 0.3 collective-permute-start.4
  10.9 0.0 collective-permute-done.15.refs_18_
  10.9 1.8 %collective-permute-start.3 = (bf16[440,128]{1,0:T(8,128)(2,1)}, bf16[440,128]{1,0:T(8,128)(2,1)S(1)}, u32[]{:S(2)}, u32[]{:S(2)}) collective-permute-start(bf16[440,128]{1,0:T(8,128)(2,1)} %bitcast.17), channel_id=1, source_target_pairs={{0,1},{1,0},{2,3},{3,2},{4,5},{5,4},{6,7},{7,6},{8,9},{9,8},{10,11... | collective-permute-start | bytes 337928 | tf_op jit(solution)/shard_map/ppermute | solution.py:72
  12.6 0.0 collective-permute-done.14.refs_17_
  12.6 2.6 %collective-permute-start = (bf16[440,128]{1,0:T(8,128)(2,1)}, bf16[440,128]{1,0:T(8,128)(2,1)S(1)}, u32[]{:S(2)}, u32[]{:S(2)}) collective-permute-start(bf16[440,128]{1,0:T(8,128)(2,1)} %bitcast.18), channel_id=1, source_target_pairs={{0,16},{1,17},{2,18},{3,19},{4,20},{5,21},{6,22},{7,23},{8,24},{9,... | collective-permute-start | bytes 337928 | tf_op jit(solution)/shard_map/ppermute | solution.py:72
  15.2 0.0 collective-permute-done.6.refs_8_
  15.2 1.6 %collective-permute-start.1 = (bf16[440,128]{1,0:T(8,128)(2,1)}, bf16[440,128]{1,0:T(8,128)(2,1)S(1)}, u32[]{:S(2)}, u32[]{:S(2)}) collective-permute-start(bf16[440,128]{1,0:T(8,128)(2,1)} %bitcast.19), channel_id=1, source_target_pairs={{0,8},{1,9},{2,10},{3,11},{4,12},{5,13},{6,14},{7,15},{8,0},{9,1},... | collective-permute-start | bytes 337928 | tf_op jit(solution)/shard_map/ppermute | solution.py:72
  16.8 0.0 collective-permute-done.5.refs_7_
  16.8 0.0 collective-permute-start.9
  16.8 0.0 collective-permute-done.4.refs_6_
  16.8 0.5 %collective-permute-start.8 = (bf16[440,128]{1,0:T(8,128)(2,1)S(1)}, bf16[440,128]{1,0:T(8,128)(2,1)S(1)}, u32[]{:S(2)}, u32[]{:S(2)}) collective-permute-start(bf16[440,128]{1,0:T(8,128)(2,1)S(1)} %collective-permute-done.4.refs_6_), channel_id=1, source_target_pairs={{0,2},{1,3},{2,0},{3,1},{4,6},{5,7},{6,4},{7,5},{8,10},{9,11},{10,... | collective-permute-start | bytes 337928 | tf_op jit(solution)/shard_map/ppermute | solution.py:72
  17.3 0.3 collective-permute-done.3.refs_5_
  17.7 0.0 collective-permute-start.7
  17.7 2.8 %collective-permute-done.refs_1_ = bf16[440,128]{1,0:T(8,128)(2,1)S(1)} collective-permute-done((bf16[440,128]{1,0:T(8,128)(2,1)}, bf16[440,128]{1,0:T(8,128)(2,1)S(1)}, u32[]{:S(2)}, u32[]{:S(2)}) %collective-permute-start) | collective-permute-done | bytes 112672 | tf_op jit(solution)/shard_map/ppermute | solution.py:72
  20.5 0.7 %collective-permute-start.2 = (bf16[440,128]{1,0:T(8,128)(2,1)S(1)}, bf16[440,128]{1,0:T(8,128)(2,1)S(1)}, u32[]{:S(2)}, u32[]{:S(2)}) collective-permute-start(bf16[440,128]{1,0:T(8,128)(2,1)S(1)} %collective-permute-done.refs_1_), channel_id=1, source_target_pairs={{0,8},{1,9},{2,10},{3,11},{4,12},{5,13},{6,14},{7,15},{8,0},{9,1},... | collective-permute-start | bytes 337928 | tf_op jit(solution)/shard_map/ppermute | solution.py:72
  21.1 0.0 collective-permute-done.1.refs_2_
  21.1 0.0 collective-permute-done.9.refs_11_
  21.1 0.0 collective-permute-done.8.refs_10_
  21.1 0.0 collective-permute-done.7.refs_9_
  21.1 4.1 %collective-permute-done.2.refs_3_ = bf16[440,128]{1,0:T(8,128)(2,1)S(1)} collective-permute-done((bf16[440,128]{1,0:T(8,128)(2,1)S(1)}, bf16[440,128]{1,0:T(8,128)(2,1)S(1)}, u32[]{:S(2)}, u32[]{:S(2)}) %collective-permute-start.2) | collective-permute-done | bytes 112672 | tf_op jit(solution)/shard_map/ppermute | solution.py:72
  25.2 0.0 copy-start
  25.2 0.9 %copy-done = bf16[128,440]{0,1:T(8,128)(2,1)S(1)} copy-done((bf16[128,440]{0,1:T(8,128)(2,1)S(1)}, bf16[128,440]{0,1:T(8,128)(2,1)}, u32[]{:S(2)}) %copy-start) | copy-done | bytes 112664
  26.1 0.0 copy-start.1
  26.1 0.8 %copy-done.1 = bf16[128,144]{0,1:T(8,128)(2,1)S(1)} copy-done((bf16[128,144]{0,1:T(8,128)(2,1)S(1)}, bf16[128,144]{0,1:T(8,128)(2,1)}, u32[]{:S(2)}) %copy-start.1) | copy-done | bytes 36888
  26.9 0.0 copy-start.2
  26.9 1.7 %products.1 = (f32[144,128]{1,0:T(8,128)S(1)}, bf16[144,128]{1,0:T(8,128)(2,1)S(1)}, bf16[144,128]{1,0:T(8,128)(2,1)S(1)}, bf16[144,128]{1,0:T(8,128)(2,1)S(1)}) custom-call(bf16[440,128]{1,0:T(8,128)(2,1)S(1)} %bitcast.20, bf16[440,128]{1,0:T(8,128)(2,1)S(1)} %collective-permute-done.refs_1_, bf16[440,128]{1,0:T(8,128)(2,1)S(1)} %collective-permute-done.1.refs_2_, ...), custom_call_target="tpu_custom_call" | custom-call | tf_op jit(solution)/shard_map/products/pallas_call | solution.py:58
  28.6 2.0 %collective-permute-start.17 = (bf16[144,128]{1,0:T(8,128)(2,1)S(1)}, bf16[144,128]{1,0:T(8,128)(2,1)S(1)}, u32[]{:S(2)}, u32[]{:S(2)}) collective-permute-start(bf16[144,128]{1,0:T(8,128)(2,1)S(1)} %get-tuple-element.10), channel_id=1, source_target_pairs={{0,16},{1,17},{2,18},{3,19},{4,20},{5,21},{6,22},{7,23},{8,24},{9,... | collective-permute-start | bytes 110600 | tf_op jit(solution)/shard_map/ppermute | solution.py:72
  30.6 2.0 %collective-permute-start.18 = (bf16[144,128]{1,0:T(8,128)(2,1)S(1)}, bf16[144,128]{1,0:T(8,128)(2,1)S(1)}, u32[]{:S(2)}, u32[]{:S(2)}) collective-permute-start(bf16[144,128]{1,0:T(8,128)(2,1)S(1)} %get-tuple-element.11), channel_id=1, source_target_pairs={{0,8},{1,9},{2,10},{3,11},{4,12},{5,13},{6,14},{7,15},{8,0},{9,1},... | collective-permute-start | bytes 110600 | tf_op jit(solution)/shard_map/ppermute | solution.py:72
  32.6 0.5 %collective-permute-start.19 = (bf16[144,128]{1,0:T(8,128)(2,1)S(1)}, bf16[144,128]{1,0:T(8,128)(2,1)S(1)}, u32[]{:S(2)}, u32[]{:S(2)}) collective-permute-start(bf16[144,128]{1,0:T(8,128)(2,1)S(1)} %get-tuple-element.12), channel_id=1, source_target_pairs={{0,24},{1,25},{2,26},{3,27},{4,28},{5,29},{6,30},{7,31},{8,16},{9,... | collective-permute-start | bytes 110600 | tf_op jit(solution)/shard_map/ppermute | solution.py:72
  33.0 0.5 %collective-permute-done.17 = bf16[144,128]{1,0:T(8,128)(2,1)S(1)} collective-permute-done((bf16[144,128]{1,0:T(8,128)(2,1)S(1)}, bf16[144,128]{1,0:T(8,128)(2,1)S(1)}, u32[]{:S(2)}, u32[]{:S(2)}) %collective-permute-start.17) | collective-permute-done | bytes 36896 | tf_op jit(solution)/shard_map/ppermute | solution.py:72
  33.5 1.0 %collective-permute-done.18 = bf16[144,128]{1,0:T(8,128)(2,1)S(1)} collective-permute-done((bf16[144,128]{1,0:T(8,128)(2,1)S(1)}, bf16[144,128]{1,0:T(8,128)(2,1)S(1)}, u32[]{:S(2)}, u32[]{:S(2)}) %collective-permute-start.18) | collective-permute-done | bytes 36896 | tf_op jit(solution)/shard_map/ppermute | solution.py:72
  34.5 3.8 %collective-permute-done.19 = bf16[144,128]{1,0:T(8,128)(2,1)S(1)} collective-permute-done((bf16[144,128]{1,0:T(8,128)(2,1)S(1)}, bf16[144,128]{1,0:T(8,128)(2,1)S(1)}, u32[]{:S(2)}, u32[]{:S(2)}) %collective-permute-start.19) | collective-permute-done | bytes 36896 | tf_op jit(solution)/shard_map/ppermute | solution.py:72
  38.3 0.0 copy-done.2
  38.3 0.7 %fusion.3 = f32[128,144]{0,1:T(8,128)} fusion(f32[144,128]{1,0:T(8,128)S(1)} %get-tuple-element.9, f32[128,144]{0,1:T(8,128)S(1)} %copy-done.2, bf16[144,128]{1,0:T(8,128)(2,1)S(1)} %collective-permute-done.19, bf16[144,128]{1,0:T(8,128)(2,1)S(1)} %collective-permute-done.18, bf16[144,128]{1,0:T(8,128)(2,1)S(1)} %collective-permute-done.17), kind=kLoop, calls=%fused_computation.4 | loop fusion | flops 129024 | bytes 331776 | tf_op jit(solution)/shard_map/transpose | solution.py:95
Async XLA Ops:
  0.0 6.1 %collective-permute-start.12 = (bf16[144,128]{1,0:T(8,128)(2,1)}, bf16[144,128]{1,0:T(8,128)(2,1)S(1)}, u32[]{:S(2)}, u32[]{:S(2)}) collective-permute-start(bf16[144,128]{1,0:T(8,128)(2,1)} %bitcast.22), channel_id=1, source_target_pairs={{0,5},{1,4},{2,7},{3,6},{4,1},{5,0},{6,3},{7,2},{8,13},{9,12},{10,... | collective-permute-start | bytes 110600 | tf_op jit(solution)/shard_map/ppermute | solution.py:72
  3.9 4.2 %collective-permute-start.11 = (bf16[144,128]{1,0:T(8,128)(2,1)}, bf16[144,128]{1,0:T(8,128)(2,1)S(1)}, u32[]{:S(2)}, u32[]{:S(2)}) collective-permute-start(bf16[144,128]{1,0:T(8,128)(2,1)} %bitcast.23), channel_id=1, source_target_pairs={{0,4},{1,5},{2,6},{3,7},{4,0},{5,1},{6,2},{7,3},{8,12},{9,13},{10,... | collective-permute-start | bytes 110600 | tf_op jit(solution)/shard_map/ppermute | solution.py:72
  4.5 4.2 %collective-permute-start.10 = (bf16[144,128]{1,0:T(8,128)(2,1)}, bf16[144,128]{1,0:T(8,128)(2,1)S(1)}, u32[]{:S(2)}, u32[]{:S(2)}) collective-permute-start(bf16[144,128]{1,0:T(8,128)(2,1)} %bitcast.24), channel_id=1, source_target_pairs={{0,1},{1,0},{2,3},{3,2},{4,5},{5,4},{6,7},{7,6},{8,9},{9,8},{10,11... | collective-permute-start | bytes 110600 | tf_op jit(solution)/shard_map/ppermute | solution.py:72
  4.5 4.7 %collective-permute-start.13 = (bf16[144,128]{1,0:T(8,128)(2,1)}, bf16[144,128]{1,0:T(8,128)(2,1)S(1)}, u32[]{:S(2)}, u32[]{:S(2)}) collective-permute-start(bf16[144,128]{1,0:T(8,128)(2,1)} %bitcast.25), channel_id=1, source_target_pairs={{0,2},{1,3},{2,0},{3,1},{4,6},{5,7},{6,4},{7,5},{8,10},{9,11},{10,... | collective-permute-start | bytes 110600 | tf_op jit(solution)/shard_map/ppermute | solution.py:72
  6.1 4.5 %collective-permute-start.16 = (bf16[144,128]{1,0:T(8,128)(2,1)S(1)}, bf16[144,128]{1,0:T(8,128)(2,1)S(1)}, u32[]{:S(2)}, u32[]{:S(2)}) collective-permute-start(bf16[144,128]{1,0:T(8,128)(2,1)S(1)} %collective-permute-done.12.refs_15_), channel_id=1, source_target_pairs={{0,2},{1,3},{2,0},{3,1},{4,6},{5,7},{6,4},{7,5},{8,10},{9,11},{10,... | collective-permute-start | bytes 110600 | tf_op jit(solution)/shard_map/ppermute | solution.py:72
  8.1 2.8 %collective-permute-start.15 = (bf16[144,128]{1,0:T(8,128)(2,1)S(1)}, bf16[144,128]{1,0:T(8,128)(2,1)S(1)}, u32[]{:S(2)}, u32[]{:S(2)}) collective-permute-start(bf16[144,128]{1,0:T(8,128)(2,1)S(1)} %collective-permute-done.11.refs_14_), channel_id=1, source_target_pairs={{0,2},{1,3},{2,0},{3,1},{4,6},{5,7},{6,4},{7,5},{8,10},{9,11},{10,... | collective-permute-start | bytes 110600 | tf_op jit(solution)/shard_map/ppermute | solution.py:72
  8.6 4.0 %collective-permute-start.14 = (bf16[144,128]{1,0:T(8,128)(2,1)S(1)}, bf16[144,128]{1,0:T(8,128)(2,1)S(1)}, u32[]{:S(2)}, u32[]{:S(2)}) collective-permute-start(bf16[144,128]{1,0:T(8,128)(2,1)S(1)} %collective-permute-done.10.refs_13_), channel_id=1, source_target_pairs={{0,2},{1,3},{2,0},{3,1},{4,6},{5,7},{6,4},{7,5},{8,10},{9,11},{10,... | collective-permute-start | bytes 110600 | tf_op jit(solution)/shard_map/ppermute | solution.py:72
  8.6 6.6 %collective-permute-start.6 = (bf16[440,128]{1,0:T(8,128)(2,1)}, bf16[440,128]{1,0:T(8,128)(2,1)S(1)}, u32[]{:S(2)}, u32[]{:S(2)}) collective-permute-start(bf16[440,128]{1,0:T(8,128)(2,1)} %bitcast.14), channel_id=1, source_target_pairs={{0,2},{1,3},{2,0},{3,1},{4,6},{5,7},{6,4},{7,5},{8,10},{9,11},{10,... | collective-permute-start | bytes 337928 | tf_op jit(solution)/shard_map/ppermute | solution.py:72
  9.1 7.7 %collective-permute-start.5 = (bf16[440,128]{1,0:T(8,128)(2,1)}, bf16[440,128]{1,0:T(8,128)(2,1)S(1)}, u32[]{:S(2)}, u32[]{:S(2)}) collective-permute-start(bf16[440,128]{1,0:T(8,128)(2,1)} %bitcast.15), channel_id=1, source_target_pairs={{0,5},{1,4},{2,7},{3,6},{4,1},{5,0},{6,3},{7,2},{8,13},{9,12},{10,... | collective-permute-start | bytes 337928 | tf_op jit(solution)/shard_map/ppermute | solution.py:72
  10.6 6.2 %collective-permute-start.4 = (bf16[440,128]{1,0:T(8,128)(2,1)}, bf16[440,128]{1,0:T(8,128)(2,1)S(1)}, u32[]{:S(2)}, u32[]{:S(2)}) collective-permute-start(bf16[440,128]{1,0:T(8,128)(2,1)} %bitcast.16), channel_id=1, source_target_pairs={{0,4},{1,5},{2,6},{3,7},{4,0},{5,1},{6,2},{7,3},{8,12},{9,13},{10,... | collective-permute-start | bytes 337928 | tf_op jit(solution)/shard_map/ppermute | solution.py:72
  10.9 6.8 %collective-permute-start.3 = (bf16[440,128]{1,0:T(8,128)(2,1)}, bf16[440,128]{1,0:T(8,128)(2,1)S(1)}, u32[]{:S(2)}, u32[]{:S(2)}) collective-permute-start(bf16[440,128]{1,0:T(8,128)(2,1)} %bitcast.17), channel_id=1, source_target_pairs={{0,1},{1,0},{2,3},{3,2},{4,5},{5,4},{6,7},{7,6},{8,9},{9,8},{10,11... | collective-permute-start | bytes 337928 | tf_op jit(solution)/shard_map/ppermute | solution.py:72
  12.6 7.8 %collective-permute-start = (bf16[440,128]{1,0:T(8,128)(2,1)}, bf16[440,128]{1,0:T(8,128)(2,1)S(1)}, u32[]{:S(2)}, u32[]{:S(2)}) collective-permute-start(bf16[440,128]{1,0:T(8,128)(2,1)} %bitcast.18), channel_id=1, source_target_pairs={{0,16},{1,17},{2,18},{3,19},{4,20},{5,21},{6,22},{7,23},{8,24},{9,... | collective-permute-start | bytes 337928 | tf_op jit(solution)/shard_map/ppermute | solution.py:72
  15.2 5.9 %collective-permute-start.1 = (bf16[440,128]{1,0:T(8,128)(2,1)}, bf16[440,128]{1,0:T(8,128)(2,1)S(1)}, u32[]{:S(2)}, u32[]{:S(2)}) collective-permute-start(bf16[440,128]{1,0:T(8,128)(2,1)} %bitcast.19), channel_id=1, source_target_pairs={{0,8},{1,9},{2,10},{3,11},{4,12},{5,13},{6,14},{7,15},{8,0},{9,1},... | collective-permute-start | bytes 337928 | tf_op jit(solution)/shard_map/ppermute | solution.py:72
  16.8 4.3 %collective-permute-start.9 = (bf16[440,128]{1,0:T(8,128)(2,1)S(1)}, bf16[440,128]{1,0:T(8,128)(2,1)S(1)}, u32[]{:S(2)}, u32[]{:S(2)}) collective-permute-start(bf16[440,128]{1,0:T(8,128)(2,1)S(1)} %collective-permute-done.5.refs_7_), channel_id=1, source_target_pairs={{0,2},{1,3},{2,0},{3,1},{4,6},{5,7},{6,4},{7,5},{8,10},{9,11},{10,... | collective-permute-start | bytes 337928 | tf_op jit(solution)/shard_map/ppermute | solution.py:72
  16.8 4.3 %collective-permute-start.8 = (bf16[440,128]{1,0:T(8,128)(2,1)S(1)}, bf16[440,128]{1,0:T(8,128)(2,1)S(1)}, u32[]{:S(2)}, u32[]{:S(2)}) collective-permute-start(bf16[440,128]{1,0:T(8,128)(2,1)S(1)} %collective-permute-done.4.refs_6_), channel_id=1, source_target_pairs={{0,2},{1,3},{2,0},{3,1},{4,6},{5,7},{6,4},{7,5},{8,10},{9,11},{10,... | collective-permute-start | bytes 337928 | tf_op jit(solution)/shard_map/ppermute | solution.py:72
  17.7 3.5 %collective-permute-start.7 = (bf16[440,128]{1,0:T(8,128)(2,1)S(1)}, bf16[440,128]{1,0:T(8,128)(2,1)S(1)}, u32[]{:S(2)}, u32[]{:S(2)}) collective-permute-start(bf16[440,128]{1,0:T(8,128)(2,1)S(1)} %collective-permute-done.3.refs_5_), channel_id=1, source_target_pairs={{0,2},{1,3},{2,0},{3,1},{4,6},{5,7},{6,4},{7,5},{8,10},{9,11},{10,... | collective-permute-start | bytes 337928 | tf_op jit(solution)/shard_map/ppermute | solution.py:72
  20.5 4.8 %collective-permute-start.2 = (bf16[440,128]{1,0:T(8,128)(2,1)S(1)}, bf16[440,128]{1,0:T(8,128)(2,1)S(1)}, u32[]{:S(2)}, u32[]{:S(2)}) collective-permute-start(bf16[440,128]{1,0:T(8,128)(2,1)S(1)} %collective-permute-done.refs_1_), channel_id=1, source_target_pairs={{0,8},{1,9},{2,10},{3,11},{4,12},{5,13},{6,14},{7,15},{8,0},{9,1},... | collective-permute-start | bytes 337928 | tf_op jit(solution)/shard_map/ppermute | solution.py:72
  25.2 0.9 %copy-start = (bf16[128,440]{0,1:T(8,128)(2,1)S(1)}, bf16[128,440]{0,1:T(8,128)(2,1)}, u32[]{:S(2)}) copy-start(bf16[128,440]{0,1:T(8,128)(2,1)} %param.3) | copy-start | bytes 337924
  26.1 0.8 %copy-start.1 = (bf16[128,144]{0,1:T(8,128)(2,1)S(1)}, bf16[128,144]{0,1:T(8,128)(2,1)}, u32[]{:S(2)}) copy-start(bf16[128,144]{0,1:T(8,128)(2,1)} %param.4) | copy-start | bytes 110596
  26.9 11.4 %copy-start.2 = (f32[128,144]{0,1:T(8,128)S(1)}, f32[128,144]{0,1:T(8,128)}, u32[]{:S(2)}) copy-start(f32[128,144]{0,1:T(8,128)} %param.5) | copy-start | bytes 221188
  28.6 4.9 %collective-permute-start.17 = (bf16[144,128]{1,0:T(8,128)(2,1)S(1)}, bf16[144,128]{1,0:T(8,128)(2,1)S(1)}, u32[]{:S(2)}, u32[]{:S(2)}) collective-permute-start(bf16[144,128]{1,0:T(8,128)(2,1)S(1)} %get-tuple-element.10), channel_id=1, source_target_pairs={{0,16},{1,17},{2,18},{3,19},{4,20},{5,21},{6,22},{7,23},{8,24},{9,... | collective-permute-start | bytes 110600 | tf_op jit(solution)/shard_map/ppermute | solution.py:72
  30.6 4.0 %collective-permute-start.18 = (bf16[144,128]{1,0:T(8,128)(2,1)S(1)}, bf16[144,128]{1,0:T(8,128)(2,1)S(1)}, u32[]{:S(2)}, u32[]{:S(2)}) collective-permute-start(bf16[144,128]{1,0:T(8,128)(2,1)S(1)} %get-tuple-element.11), channel_id=1, source_target_pairs={{0,8},{1,9},{2,10},{3,11},{4,12},{5,13},{6,14},{7,15},{8,0},{9,1},... | collective-permute-start | bytes 110600 | tf_op jit(solution)/shard_map/ppermute | solution.py:72
  32.6 5.8 %collective-permute-start.19 = (bf16[144,128]{1,0:T(8,128)(2,1)S(1)}, bf16[144,128]{1,0:T(8,128)(2,1)S(1)}, u32[]{:S(2)}, u32[]{:S(2)}) collective-permute-start(bf16[144,128]{1,0:T(8,128)(2,1)S(1)} %get-tuple-element.12), channel_id=1, source_target_pairs={{0,24},{1,25},{2,26},{3,27},{4,28},{5,29},{6,30},{7,31},{8,16},{9,... | collective-permute-start | bytes 110600 | tf_op jit(solution)/shard_map/ppermute | solution.py:72
